TPU v7x, 768 devices: a whole 4x8x12 slice. The times are simulated.
768 devices in a mesh: dp: 128 (over x, y, z_lo), tensor: 6 (over z_hi, core).
Axes of the slice: x: 4, y: 8, z: 12 (z_hi: 3, z_lo: 4; z = z_hi * 4 + z_lo), core: 2. Of those that a mesh axis runs over, the one named last changes fastest.
Arguments:
- latent_raw: bfloat16 [24576, 512], P('dp'), may hold values from -24 to 24
- norm_gain: float32 [512], replicated, may hold values from 0.5 to 1.5
- up_weight: bfloat16 [512, 24576], P(None, 'tensor'), may hold values from -0.25 to 0.25
- grad_kv: bfloat16 [24576, 24576], P('dp', 'tensor'), may hold values from -3 to 3
Outputs:
- latent_grad: bfloat16 [24576, 512], P('dp')
- gain_grad: float32 [512], replicated
- weight_grad: float32 [512, 24576], P('dp', 'tensor')
All inputs are finite; a program needn't handle non-finite values.
Results may differ from a plain program's by a relative error of at most 0.0029.
Values may be sent and summed in bfloat16 or wider, within the bound.
A program may use at most 64 MiB of HBM per device.

v0:
```python
import functools

import jax
import jax.numpy as jnp
from jax import lax
from jax.sharding import Mesh
from jax.sharding import PartitionSpec as P

DP = ("dp_0", "dp_1", "dp_2")
TENSOR = ("tensor_0", "tensor_1")
DP_TENSOR = ("dp_0", "dp_1", "dp_2", "tensor_0", "tensor_1")


epsilon = 1e-06


def cut_along(shard, dim, count):
    before, after = (shard.shape[:dim], shard.shape[dim + 1 :])
    return jnp.moveaxis(shard.reshape(*before, count, -1, *after), dim, 0)


def sum_at_owner(shard, axis, dim):
    count = lax.axis_size(axis)
    pieces = lax.all_to_all(cut_along(shard, dim, count), axis, 0, 0, tiled=True)
    return jnp.sum(pieces, axis=0)


def laid_out(pieces, dim):
    pieces = jnp.moveaxis(pieces, 0, dim)
    shape = pieces.shape
    return pieces.reshape(*shape[:dim], shape[dim] * shape[dim + 1], *shape[dim + 2 :])


def copy_for_each(shard, axis):
    copies = jnp.broadcast_to(shard, (lax.axis_size(axis), *shard.shape))
    return lax.all_to_all(copies, axis, split_axis=0, concat_axis=0, tiled=True)


def gather_directly(shard, axis, dim):
    return laid_out(copy_for_each(shard, axis), dim)


def one_axis_at_a_time(shard, axes):
    return functools.reduce(lax.psum, axes, shard)


def scatter_lines(shard, axis, dim):
    count = lax.axis_size(axis)
    pieces = cut_along(shard, dim, count)
    lines = pieces.reshape(count, -1)
    width = max(16, -(-lines.shape[1] // 1024) * 8)
    lines = jnp.pad(lines, ((0, 0), (0, width * 128 - lines.shape[1]))).reshape(-1, 128)
    own = lax.psum_scatter(lines, axis, scatter_dimension=0, tiled=True)
    return own.reshape(-1)[: pieces[0].size].reshape(pieces.shape[1:])


def normalize(latent_raw):
    latent_full = latent_raw.astype(jnp.float32)
    inverse = lax.rsqrt(jnp.mean(latent_full * latent_full, axis=-1, keepdims=True) + epsilon)
    return (latent_full * inverse, inverse)


def norm_backward(grad_norm, scaled_rows, inverse, norm_gain):
    upstream = grad_norm * norm_gain
    centred = upstream - scaled_rows * jnp.mean(upstream * scaled_rows, axis=-1, keepdims=True)
    return (inverse * centred).astype(jnp.bfloat16)


def per_device(latent_raw, norm_gain, up_weight, grad_kv):
    scaled_rows, inverse = normalize(latent_raw)
    normed = (scaled_rows * norm_gain).astype(jnp.bfloat16)
    factor = float(latent_raw.shape[0] * lax.axis_size(DP)) ** (-0.5)
    partial_norm = lax.dot_general(
        grad_kv, up_weight, (((1,), (1,)), ((), ())), preferred_element_type=jnp.float32
    )
    grad_norm = sum_at_owner(partial_norm, TENSOR, 0)
    row_count = grad_norm.shape[0]
    offset = lax.axis_index(TENSOR) * row_count
    scaled_part = lax.dynamic_slice_in_dim(scaled_rows, offset, row_count, 0)
    inverse_part = lax.dynamic_slice_in_dim(inverse, offset, row_count, 0)
    gain_local = jnp.sum(grad_norm * scaled_part, axis=0)
    latent_part = norm_backward(grad_norm, scaled_part, inverse_part, norm_gain)
    latent_grad = gather_directly(latent_part, TENSOR, 0)
    gain_grad = one_axis_at_a_time(gain_local, DP_TENSOR) * factor
    weight_partial = lax.dot_general(
        normed, grad_kv, (((0,), (0,)), ((), ())), preferred_element_type=jnp.float32
    )
    weight_grad = scatter_lines(weight_partial, DP, 0) * factor
    return (latent_grad, gain_grad, weight_grad)


def solution(mesh):
    split = Mesh(
        mesh.devices.reshape(4, 8, 4, 3, 2), ("dp_0", "dp_1", "dp_2", "tensor_0", "tensor_1")
    )
    in_specs = (P(DP, None), P(), P(None, TENSOR), P(DP, TENSOR))
    out_specs = (P(DP, None), P(), P(DP, TENSOR))
    return jax.shard_map(
        per_device, mesh=split, in_specs=in_specs, out_specs=out_specs, check_vma=False
    )
```

profile of v0, /device:TPU:256, one launch (start us, length us, event | category | flops | bytes accessed | tf_op | source)
XLA Modules:
  0.0 809.4 jit_solution(7588429570986653251)
XLA Ops:
  7.2 0.0 reduce-scatter.2.cloned.1.call-start
  7.2 1.2 fusion
  8.4 0.3 copy-done
  8.7 5.5 fusion.1
  14.2 9.3 %reshape.48 = f32[16384,128]{1,0:T(8,128)} reshape(f32[512,4096]{1,0:T(8,128)} %fusion.1) | data formatting | bytes 16777216 | tf_op jit(solution)/shard_map/reshape | solution.py:52
  23.5 4.5 fusion.3
  28.1 10.8 %all-to-all-start = ((f32[6,32,512]{2,1,0:T(8,128)}), f32[6,32,512]{2,1,0:T(8,128)S(1)}, u32[]{:S(2)}, u32[]{:S(2)}) async-start(f32[6,32,512]{2,1,0:T(8,128)} %bitcast), calls=%async_computation | async-start | bytes 786432 | tf_op jit(solution)/shard_map/all_to_all | solution.py:24
  38.9 0.1 dynamic-slice.3
  39.0 0.1 convert_multiply_fusion
  39.1 10.7 %all-to-all-done = f32[6,32,512]{2,1,0:T(8,128)S(1)} async-done(((f32[6,32,512]{2,1,0:T(8,128)}), f32[6,32,512]{2,1,0:T(8,128)S(1)}, u32[]{:S(2)}, u32[]{:S(2)}) %all-to-all-start) | async-done | bytes 393248 | tf_op jit(solution)/shard_map/all_to_all | solution.py:24
  49.9 0.1 multiply_reduce_fusion
  50.0 0.1 multiply_convert_fusion.2
  50.1 0.7 broadcast_in_dim.2
  50.8 11.7 %all-to-all-start.1 = ((bf16[6,32,512]{2,1,0:T(8,128)(2,1)}), bf16[6,32,512]{2,1,0:T(8,128)(2,1)S(1)}, u32[]{:S(2)}, u32[]{:S(2)}) async-start(bf16[6,32,512]{2,1,0:T(8,128)(2,1)} %broadcast_in_dim.2), calls=%async_computation.1 | async-start | bytes 393216 | tf_op jit(solution)/shard_map/all_to_all | solution.py:36
  62.5 10.5 %psum.35 = f32[512]{0:T(512)S(1)} all-reduce(f32[512]{0:T(512)S(1)} %get-tuple-element.3), channel_id=1, replica_groups=mesh['dp_0'=4,'dp_1'=8,'dp_2'=4,'tensor_0'=3,'tensor_1'=2] {'dp_0'}, use_global_device_ids=true, to_apply=%region_4.0 | all-reduce | flops 512 | bytes 4096 | tf_op jit(solution)/shard_map/psum | solution.py:44
  73.0 17.6 %psum.36 = f32[512]{0:T(512)S(1)} all-reduce(f32[512]{0:T(512)S(1)} %psum.35), channel_id=1, replica_groups=mesh['dp_0'=4,'dp_1'=8,'dp_2'=4,'tensor_0'=3,'tensor_1'=2] {'dp_1'}, use_global_device_ids=true, to_apply=%region_5.0 | all-reduce | flops 512 | bytes 4096 | tf_op jit(solution)/shard_map/psum | solution.py:44
  90.6 11.2 %psum.37 = f32[512]{0:T(512)S(1)} all-reduce(f32[512]{0:T(512)S(1)} %psum.36), channel_id=1, replica_groups=mesh['dp_0'=4,'dp_1'=8,'dp_2'=4,'tensor_0'=3,'tensor_1'=2] {'dp_2'}, use_global_device_ids=true, to_apply=%region_6.0 | all-reduce | flops 512 | bytes 4096 | tf_op jit(solution)/shard_map/psum | solution.py:44
  101.8 8.9 %psum.38 = f32[512]{0:T(512)S(1)} all-reduce(f32[512]{0:T(512)S(1)} %psum.37), channel_id=1, replica_groups=mesh['dp_0'=4,'dp_1'=8,'dp_2'=4,'tensor_0'=3,'tensor_1'=2] {'tensor_0'}, use_global_device_ids=true, to_apply=%region_7.0 | all-reduce | flops 512 | bytes 4096 | tf_op jit(solution)/shard_map/psum | solution.py:44
  110.6 2.5 psum.39
  113.1 0.6 broadcast_multiply_fusion.1
  113.7 686.7 %reduce-scatter.2.cloned.1.call-done = f32[128,128]{1,0:T(8,128)} async-done(((f32[16384,128]{1,0:T(8,128)}), f32[128,128]{1,0:T(8,128)}) %reduce-scatter.2.cloned.1.call-update) | async-done | bytes 65552 | tf_op jit(solution)/shard_map/reduce_scatter | solution.py:53
  800.4 0.8 broadcast_multiply_fusion
  801.2 0.7 mul.89
  801.9 0.7 copy.8
  (10 shorter events, 0.1 us)
Async XLA Ops:
  7.2 1.5 copy-start
  7.2 793.2 %reduce-scatter.2.cloned.1.call-start = ((), (), s32[]{:S(2)}) async-start(), calls=%async_computation.3 | async-start | bytes 8454144 | tf_op jit(solution)/shard_map/reduce_scatter | solution.py:53
  23.5 15.5 %copy-start.1 = (bf16[192,512]{1,0:T(8,128)(2,1)S(1)}, bf16[192,512]{1,0:T(8,128)(2,1)}, u32[]{:S(2)}) copy-start(bf16[192,512]{1,0:T(8,128)(2,1)} %param.4) | copy-start | bytes 589828
  23.5 26.3 %copy-start.2 = (f32[512]{0:T(512)S(1)}, f32[512]{0:T(512)}, u32[]{:S(2)}) copy-start(f32[512]{0:T(512)} %param.5) | copy-start | bytes 6148
  28.1 21.7 %all-to-all-start = ((f32[6,32,512]{2,1,0:T(8,128)}), f32[6,32,512]{2,1,0:T(8,128)S(1)}, u32[]{:S(2)}, u32[]{:S(2)}) async-start(f32[6,32,512]{2,1,0:T(8,128)} %bitcast), calls=%async_computation | async-start | bytes 786432 | tf_op jit(solution)/shard_map/all_to_all | solution.py:24
  50.8 62.9 %all-to-all-start.1 = ((bf16[6,32,512]{2,1,0:T(8,128)(2,1)}), bf16[6,32,512]{2,1,0:T(8,128)(2,1)S(1)}, u32[]{:S(2)}, u32[]{:S(2)}) async-start(bf16[6,32,512]{2,1,0:T(8,128)(2,1)} %broadcast_in_dim.2), calls=%async_computation.1 | async-start | bytes 393216 | tf_op jit(solution)/shard_map/all_to_all | solution.py:36
Sparse Core Ops, SparseCore 0:
  23.6 776.7 reduce-scatter.1
where the time goes:
time: 810 us; the launch traced here: 809 us
  waiting for transfers between devices  697 us (86%)
  blocking collectives  50.6 us (6%)
  starting transfers between devices  22.6 us (3%)
  between operations  14.1 us (2%)
  local copies, waits for them, and re-layouts  11.7 us (1%)
  matrix products  10.1 us (1%)
    reduce_scatter x1, waiting for transfers between devices, scatter_lines(): own = lax.psum_scatter(lines, axis, scatter_dimension=0, tiled=True)  687 us
    psum x5, blocking collectives, one_axis_at_a_time(): return functools.reduce(lax.psum, axes, shard)  50.6 us
  transfers between devices with their start and end apart: 3, of which 2 were waited for; matrix products, arithmetic and copies ran while one was open for 1% of the time, Pallas kernels for 0%

commit v1 on v0

v1 whole, which is shorter than its diff:
```python
import functools

import jax
import jax.numpy as jnp
from jax import lax
from jax.experimental import pallas as pl
from jax.experimental.pallas import tpu as pltpu
from jax.sharding import Mesh
from jax.sharding import PartitionSpec as P

X, Y, Z, H, C = AXES = ("dp_0", "dp_1", "dp_2", "tensor_0", "tensor_1")
DP = (X, Y, Z)
TENSOR = (H, C)
NX, NY, NZ, NH, NC = 4, 8, 4, 3, 2
NT = NH * NC
SIZE = dict(zip(AXES, (NX, NY, NZ, NH, NC)))
MESH = pl.DeviceIdType.MESH

KVL = 512
COLS = 4096
ROWS = 192
BLOCK = COLS // NX
PART = ROWS // NT
OWN = KVL // (NX * NY * NZ)
STRIP = OWN * NZ
epsilon = 1e-06

CHUNKS = ((0, 256), (256, 256), (512, 256), (768, 256))
BATCHES = ((0, 768), (768, 256))
LAST_OF_BATCH = {2: 0, 3: 1}

X_OFFSETS = (1, 3, 2)
Y_OFFSETS = (1, 7, 2, 6, 3, 5, 4)
XZ_OFFSETS = tuple((i, j) for i in range(NX) for j in range(NZ) if (i, j) != (0, 0))
T_OFFSETS = tuple((i, j) for i in range(NH) for j in range(NC) if (i, j) != (0, 0))


def shifted(axis, offset):
    return lax.rem(lax.axis_index(axis) + (offset % SIZE[axis]), SIZE[axis])


def at(**offsets):
    return {axis: shifted(axis, offset) for axis, offset in offsets.items() if offset % SIZE[axis]}


def normalize(latent):
    full = latent.astype(jnp.float32)
    inverse = lax.rsqrt(jnp.mean(full * full, axis=-1, keepdims=True) + epsilon)
    return full * inverse, inverse


def kernel(
    factor,
    latent_hbm, gain_ref, up_hbm, grad_hbm,
    latent_out, gain_out, weight_out,
    latent, up, grad, normed, tokens, full, wsend, ybuf, esend, ebuf, tsend, tbuf, lbuf,
    g1, g2, g3,
    local_sem, xs, xr, ys, yr, es, er, ts, tr, ls, lr, gs, gr,
):
    x, y, z = (lax.axis_index(a) for a in DP)
    t = lax.axis_index(H) * NC + lax.axis_index(C)
    sends = []

    def send(src, dst, send_sem, recv_sem, device):
        copy = pltpu.make_async_remote_copy(
            src_ref=src, dst_ref=dst, send_sem=send_sem, recv_sem=recv_sem,
            device_id=device, device_id_type=MESH,
        )
        copy.start()
        sends.append(copy)
        return copy

    loads = [
        pltpu.make_async_copy(latent_hbm, latent, local_sem.at[0]),
        pltpu.make_async_copy(grad_hbm, grad, local_sem.at[1]),
        pltpu.make_async_copy(
            grad_hbm.at[:, pl.ds(pl.multiple_of(x * BLOCK, BLOCK), BLOCK)],
            tokens.at[pl.ds(0, ROWS), :], local_sem.at[2],
        ),
        pltpu.make_async_copy(up_hbm, up, local_sem.at[3]),
    ]
    for load in loads:
        load.start()

    barrier = pltpu.get_barrier_semaphore()
    devices = [at(**{X: i, Z: j}) for i, j in XZ_OFFSETS]
    devices += [at(**{Y: i}) for i in Y_OFFSETS]
    devices += [at(**{H: i, C: j}) for i, j in T_OFFSETS]
    for device in devices:
        pl.semaphore_signal(barrier, inc=1, device_id=device, device_id_type=MESH)

    loads[0].wait()
    scaled, _ = normalize(latent[...])
    normed[pl.ds(0, ROWS), :] = (scaled * gain_ref[...]).astype(jnp.bfloat16)
    loads[1].wait()
    pl.semaphore_wait(barrier, len(devices))

    nsends = {}
    for n, i in enumerate(X_OFFSETS):
        nsends[i] = send(
            normed.at[pl.ds(0, ROWS), :], normed.at[pl.ds(ROWS * i, ROWS), :],
            xs.at[n, len(CHUNKS)], xr.at[n, len(CHUNKS)], at(**{X: i}),
        )
    xsends = {}
    for k, (start, width) in enumerate(CHUNKS):
        for n, i in enumerate(X_OFFSETS):
            column = pl.multiple_of(shifted(X, i) * BLOCK + start, 128)
            xsends[k, i] = send(
                grad.at[:, pl.ds(column, width)],
                tokens.at[pl.ds(ROWS * i, ROWS), pl.ds(start, width)],
                xs.at[n, k], xr.at[n, k], at(**{X: i}),
            )

    loads[3].wait()
    tsend[...] = lax.dot_general(
        grad[...], up[...], (((1,), (1,)), ((), ())), preferred_element_type=jnp.float32
    )
    tsends = []
    for n, (i, j) in enumerate(T_OFFSETS):
        other = shifted(H, i) * NC + shifted(C, j)
        tsends.append(send(
            tsend.at[pl.ds(pl.multiple_of(other * PART, PART), PART), :], tbuf.at[n],
            ts.at[n], tr.at[n], at(**{H: i, C: j}),
        ))
    loads[2].wait()

    def weight_chunk(k):
        start, width = CHUNKS[k]
        if k == 0:
            for i in X_OFFSETS:
                nsends[i].wait_recv()
        for i in X_OFFSETS:
            xsends[k, i].wait_recv()
        full[:, start : start + width] = lax.dot_general(
            normed[...], tokens[:, start : start + width], (((0,), (0,)), ((), ())),
            preferred_element_type=jnp.float32,
        )
        for q in range(NY):
            for p in range(NX):
                wsend[q, STRIP * p : STRIP * (p + 1), start : start + width] = full[
                    128 * p + STRIP * q : 128 * p + STRIP * (q + 1), start : start + width
                ].astype(jnp.bfloat16)
        copies = []
        for n, i in enumerate(Y_OFFSETS):
            copies.append(send(
                wsend.at[shifted(Y, i), :, pl.ds(start, width)],
                ybuf.at[n, :, pl.ds(start, width)],
                ys.at[n, k], yr.at[n, k], at(**{Y: i}),
            ))
        return copies

    def sum_chunk(k, copies):
        start, width = CHUNKS[k]
        for copy in copies:
            copy.wait_recv()
        for p in range(NX):
            row = pl.multiple_of(128 * p + STRIP * y, STRIP)
            total = full[pl.ds(row, STRIP), start : start + width]
            for n in range(NY - 1):
                total = total + ybuf[
                    n, STRIP * p : STRIP * (p + 1), start : start + width
                ].astype(jnp.float32)
            for q in range(NZ):
                esend[NZ * p + q, :, start : start + width] = total[OWN * q : OWN * (q + 1)]

    def exchange(b):
        start, width = BATCHES[b]
        copies = []
        for n, (i, j) in enumerate(XZ_OFFSETS):
            copies.append(send(
                esend.at[shifted(X, i) * NZ + shifted(Z, j), :, pl.ds(start, width)],
                ebuf.at[n, :, pl.ds(start, width)],
                es.at[n, b], er.at[n, b], at(**{X: i, Z: j}),
            ))
        return copies

    def latent_step():
        for copy in tsends:
            copy.wait_recv()
        own = pl.ds(pl.multiple_of(t * PART, PART), PART)
        grad_norm = tsend[own, :]
        for n in range(NT - 1):
            grad_norm = grad_norm + tbuf[n]
        scaled, inverse = normalize(latent[own, :])
        g1[t] = jnp.sum(grad_norm * scaled, axis=0, keepdims=True)
        upstream = grad_norm * gain_ref[...]
        centred = upstream - scaled * jnp.mean(upstream * scaled, axis=-1, keepdims=True)
        lbuf[own, :] = (inverse * centred).astype(jnp.bfloat16)
        copies = []
        for n, (i, j) in enumerate(T_OFFSETS):
            copies.append(send(
                g1.at[t], g1.at[t], gs.at[n], gr.at[n], at(**{H: i, C: j})
            ))
        lcopies = []
        for n, (i, j) in enumerate(T_OFFSETS):
            lcopies.append(send(
                lbuf.at[own, :], lbuf.at[own, :], ls.at[n], lr.at[n], at(**{H: i, C: j})
            ))
        return copies, lcopies

    def gain_step(copies, source, target, slot, offsets, first):
        for copy in copies:
            copy.wait_recv()
        total = source[0]
        for n in range(1, source.shape[0]):
            total = total + source[n]
        target[slot] = total
        copies = []
        for n, offset in enumerate(offsets):
            copies.append(send(
                target.at[slot], target.at[slot], gs.at[first + n], gr.at[first + n], at(**offset)
            ))
        return copies

    last = len(CHUNKS) - 1
    received = []
    pending = None
    for k in range(len(CHUNKS)):
        copies = weight_chunk(k)
        if pending is not None:
            sum_chunk(k - 1, pending)
            if k - 1 in LAST_OF_BATCH:
                received += exchange(LAST_OF_BATCH[k - 1])
        pending = copies
        if k == 1:
            gcopies, lcopies = latent_step()
        if k == last:
            gcopies = gain_step(
                gcopies, g1, g2, x * NZ + z, [{X: i, Z: j} for i, j in XZ_OFFSETS], NT - 1
            )
    sum_chunk(last, pending)
    received += exchange(LAST_OF_BATCH[last])
    gcopies = gain_step(
        gcopies, g2, g3, y, [{Y: i} for i in Y_OFFSETS], NT - 1 + NX * NZ - 1
    )
    for copy in lcopies:
        copy.wait_recv()
    latent_out[...] = lbuf[...]
    for copy in received:
        copy.wait_recv()
    for i in range(NX):
        total = None
        for j in range(NZ):
            if (i, j) == (0, 0):
                term = esend[x * NZ + z]
            else:
                term = ebuf[XZ_OFFSETS.index((i, j))]
            total = term if total is None else total + term
        column = pl.multiple_of(shifted(X, -i) * BLOCK, BLOCK)
        weight_out[:, pl.ds(column, BLOCK)] = total * factor
    for copy in gcopies:
        copy.wait_recv()
    total = g3[0]
    for n in range(1, NY):
        total = total + g3[n]
    gain_out[...] = total * factor
    for copy in sends:
        copy.wait_send()


def per_device(latent_raw, norm_gain, up_weight, grad_kv):
    factor = float(latent_raw.shape[0] * NX * NY * NZ) ** (-0.5)
    vmem = pl.BlockSpec(memory_space=pltpu.VMEM)
    hbm = pl.BlockSpec(memory_space=pl.ANY)
    dma = pltpu.SemaphoreType.DMA
    gains = NT - 1 + NX * NZ - 1 + NY - 1
    latent_grad, gain_grad, weight_grad = pl.pallas_call(
        functools.partial(kernel, factor),
        out_shape=(
            jax.ShapeDtypeStruct((ROWS, KVL), jnp.bfloat16),
            jax.ShapeDtypeStruct((1, KVL), jnp.float32),
            jax.ShapeDtypeStruct((OWN, COLS), jnp.float32),
        ),
        in_specs=[hbm, vmem, hbm, hbm],
        out_specs=(vmem, vmem, vmem),
        scratch_shapes=[
            pltpu.VMEM((ROWS, KVL), jnp.bfloat16),
            pltpu.VMEM((KVL, COLS), jnp.bfloat16),
            pltpu.VMEM((ROWS, COLS), jnp.bfloat16),
            pltpu.VMEM((NX * ROWS, KVL), jnp.bfloat16),
            pltpu.VMEM((NX * ROWS, BLOCK), jnp.bfloat16),
            pltpu.VMEM((KVL, BLOCK), jnp.float32),
            pltpu.VMEM((NY, STRIP * NX, BLOCK), jnp.bfloat16),
            pltpu.VMEM((NY - 1, STRIP * NX, BLOCK), jnp.bfloat16),
            pltpu.VMEM((NX * NZ, OWN, BLOCK), jnp.float32),
            pltpu.VMEM((NX * NZ - 1, OWN, BLOCK), jnp.float32),
            pltpu.VMEM((ROWS, KVL), jnp.float32),
            pltpu.VMEM((NT - 1, PART, KVL), jnp.float32),
            pltpu.VMEM((ROWS, KVL), jnp.bfloat16),
            pltpu.VMEM((NT, 1, KVL), jnp.float32),
            pltpu.VMEM((NX * NZ, 1, KVL), jnp.float32),
            pltpu.VMEM((NY, 1, KVL), jnp.float32),
            dma((4,)),
            dma((NX - 1, len(CHUNKS) + 1)),
            dma((NX - 1, len(CHUNKS) + 1)),
            dma((NY - 1, len(CHUNKS))),
            dma((NY - 1, len(CHUNKS))),
            dma((NX * NZ - 1, len(BATCHES))),
            dma((NX * NZ - 1, len(BATCHES))),
            dma((NT - 1,)),
            dma((NT - 1,)),
            dma((NT - 1,)),
            dma((NT - 1,)),
            dma((gains,)),
            dma((gains,)),
        ],
        compiler_params=pltpu.CompilerParams(collective_id=0, has_side_effects=True),
        name="norm_up_backward",
    )(latent_raw, norm_gain.reshape(1, KVL), up_weight, grad_kv)
    return latent_grad, gain_grad.reshape(KVL), weight_grad


def solution(mesh):
    split = Mesh(mesh.devices.reshape(NX, NY, NZ, NH, NC), AXES)
    in_specs = (P(DP, None), P(), P(None, TENSOR), P(DP, TENSOR))
    out_specs = (P(DP, None), P(), P(DP, TENSOR))
    return jax.shard_map(
        per_device, mesh=split, in_specs=in_specs, out_specs=out_specs, check_vma=False
    )
```

time: 810 us -> 73.7 us (0.09)
  the two profiles are of different devices: /device:TPU:256 before, /device:TPU:6 now
where the time goes in v1:
time: 73.7 us; the launch traced here: 73.4 us
  Pallas kernels  68.4 us (93%)
  local copies, waits for them, and re-layouts  4.34 us (6%)
    pallas_call x1, Pallas kernels, per_device(): pl.pallas_call(functools.partial(kernel, factor), out_shape=(jax.ShapeDty...  68.4 us
    unnamed x3, local copies, waits for them, and re-layouts  4.34 us

profile of v1, /device:TPU:6, one launch (start us, length us, event | category | flops | bytes accessed | tf_op | source)
XLA Modules:
  0.0 73.4 jit_solution(15275372402372988993)
XLA Ops:
  0.6 68.4 %norm_up_backward.1 = (bf16[192,512]{1,0:T(8,128)(2,1)}, f32[1,512]{1,0:T(1,128)}, f32[4,4096]{1,0:T(4,128)}) custom-call(bf16[192,512]{1,0:T(8,128)(2,1)} %latent_hbm.1, f32[1,512]{1,0:T(1,128)} %bitcast.2, bf16[512,4096]{1,0:T(8,128)(2,1)} %up_hbm.1, bf16[192,4096]{1,0:T(8,128)(2,1)} %grad_hbm.1), custom_call_target="tpu_custom_call" | custom-call | tf_op jit(solution)/shard_map/norm_up_backward/pallas_call | solution.py:267
  69.0 1.6 %copy.10 = bf16[192,512]{1,0:T(8,128)(2,1)} copy(bf16[192,512]{1,0:T(8,128)(2,1)} %get-tuple-element.12) | data formatting | bytes 393216
  70.6 1.2 %copy.11 = f32[512]{0:T(512)} copy(f32[512]{0:T(512)} %bitcast.3) | data formatting | bytes 4096
  71.9 1.5 %copy.12 = f32[4,4096]{1,0:T(4,128)} copy(f32[4,4096]{1,0:T(4,128)} %get-tuple-element.14) | data formatting | bytes 131072

commit v2 on v1

v2 whole, which is shorter than its diff:
```python
import functools

import jax
import jax.numpy as jnp
from jax import lax
from jax.experimental import pallas as pl
from jax.experimental.pallas import tpu as pltpu
from jax.sharding import Mesh
from jax.sharding import PartitionSpec as P

X, Y, Z, H, C = AXES = ("dp_0", "dp_1", "dp_2", "tensor_0", "tensor_1")
DP = (X, Y, Z)
TENSOR = (H, C)
NX, NY, NZ, NH, NC = 4, 8, 4, 3, 2
NT = NH * NC
SIZE = dict(zip(AXES, (NX, NY, NZ, NH, NC)))
MESH = pl.DeviceIdType.MESH

KVL = 512
COLS = 4096
ROWS = 192
BLOCK = COLS // NX
PART = ROWS // NT
OWN = KVL // (NX * NY * NZ)
STRIP = OWN * NZ
epsilon = 1e-06

CHUNKS = ((0, 256), (256, 256), (512, 256), (768, 128), (896, 128))
BATCHES = ((0, 512), (512, 384), (896, 128))
BATCH_AFTER = {1: 0, 3: 1, 4: 2}
SCHEDULE = "W0 W1 R0 G1 W2 R1 S0 W3 G2 W4 R2 S1 R3 R4 G3 S2 S3 S4"
HALF = ROWS // NC
PIECE = OWN * NZ * NX

X_OFFSETS = (1, 3, 2)
Y_OFFSETS = (1, 7, 2, 6, 3, 5, 4)
XZ_OFFSETS = tuple((i, j) for i in range(NX) for j in range(NZ) if (i, j) != (0, 0))
T_OFFSETS = tuple((i, j) for i in range(NH) for j in range(NC) if (i, j) != (0, 0))


def shifted(axis, offset):
    return lax.rem(lax.axis_index(axis) + (offset % SIZE[axis]), SIZE[axis])


def at(**offsets):
    return {axis: shifted(axis, offset) for axis, offset in offsets.items() if offset % SIZE[axis]}


def normalize(latent):
    full = latent.astype(jnp.float32)
    inverse = lax.rsqrt(jnp.mean(full * full, axis=-1, keepdims=True) + epsilon)
    return full * inverse, inverse


def kernel(
    factor,
    latent_hbm, gain_hbm, up_hbm, grad_hbm,
    latent_out, gain_out, weight_out,
    latent, gain, up, grad, normed, tokens, full, wsend, direct, far, farther, rsend, relayed,
    esend, ebuf, tsend, tbuf, g1, g2, g3,
    local_sem, ns, nr, fs, fr, xs, xr, ys, yr, es, er, ts, tr, ls, lr, gs, gr,
):
    x, y, z = (lax.axis_index(a) for a in DP)
    core = lax.axis_index(C)
    t = lax.axis_index(H) * NC + core
    sends = []

    def send(src, dst, send_sem, recv_sem, device):
        copy = pltpu.make_async_remote_copy(
            src_ref=src, dst_ref=dst, send_sem=send_sem, recv_sem=recv_sem,
            device_id=device, device_id_type=MESH,
        )
        copy.start()
        sends.append(copy)
        return copy

    loads = [
        pltpu.make_async_copy(latent_hbm, latent, local_sem.at[0]),
        pltpu.make_async_copy(gain_hbm, gain, local_sem.at[1]),
        pltpu.make_async_copy(grad_hbm, grad, local_sem.at[2]),
        pltpu.make_async_copy(
            grad_hbm.at[:, pl.ds(pl.multiple_of(x * BLOCK, BLOCK), BLOCK)],
            tokens.at[pl.ds(0, ROWS), :], local_sem.at[3],
        ),
        pltpu.make_async_copy(up_hbm, up, local_sem.at[4]),
    ]
    for load in loads:
        load.start()

    barrier = pltpu.get_barrier_semaphore()
    devices = [at(**{H: i, C: j}) for i, j in T_OFFSETS]
    devices += [at(**{X: i, Z: j}) for i, j in XZ_OFFSETS]
    devices += [at(**{Y: i}) for i in Y_OFFSETS]
    for device in devices:
        pl.semaphore_signal(barrier, inc=1, device_id=device, device_id_type=MESH)

    loads[0].wait()
    loads[1].wait()
    scaled, _ = normalize(latent[...])
    normed[pl.ds(0, ROWS), :] = (scaled * gain[...]).astype(jnp.bfloat16)
    pl.semaphore_wait(barrier, len(devices))

    def half(i):
        return pl.ds(pl.multiple_of(ROWS * i + HALF * core, HALF), HALF)

    halves = []
    for n, i in enumerate(X_OFFSETS):
        halves.append(send(
            normed.at[half(0), :], normed.at[half(i), :], ns.at[n], nr.at[n], at(**{X: i})
        ))
    loads[2].wait()
    xsends = {}
    for k, (start, width) in enumerate(CHUNKS):
        for n, i in enumerate(X_OFFSETS):
            column = pl.multiple_of(shifted(X, i) * BLOCK + start, 128)
            xsends[k, i] = send(
                grad.at[:, pl.ds(column, width)],
                tokens.at[pl.ds(ROWS * i, ROWS), pl.ds(start, width)],
                xs.at[n, k], xr.at[n, k], at(**{X: i}),
            )

    loads[4].wait()
    tsend[...] = lax.dot_general(
        grad[...], up[...], (((1,), (1,)), ((), ())), preferred_element_type=jnp.float32
    )
    tsends = []
    for n, (i, j) in enumerate(T_OFFSETS):
        other = shifted(H, i) * NC + shifted(C, j)
        tsends.append(send(
            tsend.at[pl.ds(pl.multiple_of(other * PART, PART), PART), :], tbuf.at[n],
            ts.at[n], tr.at[n], at(**{H: i, C: j}),
        ))
    loads[3].wait()
    forwards = []
    for n, i in enumerate(X_OFFSETS):
        halves[n].wait_recv()
        forwards.append(send(
            normed.at[half(i), :], normed.at[half(i), :], fs.at[n], fr.at[n], at(**{C: 1})
        ))

    def rows_of(other, p):
        return pl.ds(pl.multiple_of(128 * p + STRIP * other, STRIP), STRIP)

    def weight_chunk(k):
        start, width = CHUNKS[k]
        columns = slice(start, start + width)
        if k == 0:
            for copy in forwards:
                copy.wait_recv()
        for i in X_OFFSETS:
            xsends[k, i].wait_recv()
        full[:, columns] = lax.dot_general(
            normed[...], tokens[:, columns], (((0,), (0,)), ((), ())),
            preferred_element_type=jnp.float32,
        )
        for slot, offset in enumerate((3, -3, 4, 1, -1)):
            for p in range(NX):
                wsend[slot, STRIP * p : STRIP * (p + 1), columns] = full[
                    rows_of(shifted(Y, offset), p), columns
                ].astype(jnp.bfloat16)
        window = pl.ds(start, width)
        into_relay, into_total = [], []
        for side, sign in enumerate((1, -1)):
            into_relay.append(send(
                wsend.at[side, :, window], far.at[side, :, window],
                ys.at[side, k], yr.at[side, k], at(**{Y: sign}),
            ))
        for side, sign in enumerate((1, -1)):
            into_relay.append(send(
                wsend.at[2, pl.ds(PIECE // 2 * side, PIECE // 2), window],
                farther.at[side, :, window],
                ys.at[2 + side, k], yr.at[2 + side, k], at(**{Y: 2 * sign}),
            ))
        for side, sign in enumerate((1, -1)):
            into_total.append(send(
                wsend.at[3 + side, :, window], direct.at[side, :, window],
                ys.at[4 + side, k], yr.at[4 + side, k], at(**{Y: sign}),
            ))
        return into_relay, into_total

    def relay_chunk(k, into_relay):
        start, width = CHUNKS[k]
        columns = slice(start, start + width)
        for copy in into_relay:
            copy.wait_recv()
        copies = []
        for side, sign in enumerate((1, -1)):
            for p in range(NX):
                part = slice(STRIP * p, STRIP * (p + 1))
                total = full[rows_of(shifted(Y, 2 * sign), p), columns]
                total = total + far[side, part, columns].astype(jnp.float32)
                if p // 2 == side:
                    start_row = STRIP * (p - 2 * side)
                    total = total + farther[
                        side, start_row : start_row + STRIP, columns
                    ].astype(jnp.float32)
                rsend[side, part, columns] = total.astype(jnp.bfloat16)
            window = pl.ds(start, width)
            copies.append(send(
                rsend.at[side, :, window], relayed.at[side, :, window],
                ys.at[6 + side, k], yr.at[6 + side, k], at(**{Y: 2 * sign}),
            ))
        return copies

    def sum_chunk(k, copies):
        start, width = CHUNKS[k]
        columns = slice(start, start + width)
        for copy in copies:
            copy.wait_recv()
        for p in range(NX):
            part = slice(STRIP * p, STRIP * (p + 1))
            total = full[rows_of(y, p), columns]
            for source in (direct, relayed):
                for side in range(2):
                    total = total + source[side, part, columns].astype(jnp.float32)
            for q in range(NZ):
                esend[NZ * p + q, :, columns] = total[OWN * q : OWN * (q + 1)]

    def exchange(b):
        start, width = BATCHES[b]
        copies = []
        for n, (i, j) in enumerate(XZ_OFFSETS):
            copies.append(send(
                esend.at[shifted(X, i) * NZ + shifted(Z, j), :, pl.ds(start, width)],
                ebuf.at[n, :, pl.ds(start, width)],
                es.at[n, b], er.at[n, b], at(**{X: i, Z: j}),
            ))
        return copies

    def latent_step():
        for copy in tsends:
            copy.wait_recv()
        own = pl.ds(pl.multiple_of(t * PART, PART), PART)
        grad_norm = tsend[own, :]
        for n in range(NT - 1):
            grad_norm = grad_norm + tbuf[n]
        scaled, inverse = normalize(latent[own, :])
        g1[t] = jnp.sum(grad_norm * scaled, axis=0, keepdims=True)
        upstream = grad_norm * gain[...]
        centred = upstream - scaled * jnp.mean(upstream * scaled, axis=-1, keepdims=True)
        latent_out[own, :] = (inverse * centred).astype(jnp.bfloat16)
        copies = []
        for n, (i, j) in enumerate(T_OFFSETS):
            copies.append(send(
                g1.at[t], g1.at[t], gs.at[n], gr.at[n], at(**{H: i, C: j})
            ))
        lcopies = []
        for n, (i, j) in enumerate(T_OFFSETS):
            lcopies.append(send(
                latent_out.at[own, :], latent_out.at[own, :], ls.at[n], lr.at[n],
                at(**{H: i, C: j}),
            ))
        return copies, lcopies

    def gain_step(copies, source, target, slot, offsets, first):
        for copy in copies:
            copy.wait_recv()
        total = source[0]
        for n in range(1, source.shape[0]):
            total = total + source[n]
        target[slot] = total
        copies = []
        for n, offset in enumerate(offsets):
            copies.append(send(
                target.at[slot], target.at[slot], gs.at[first + n], gr.at[first + n], at(**offset)
            ))
        return copies

    into_relay, into_total, received = {}, {}, []
    gcopies = lcopies = None
    for step in SCHEDULE.split():
        kind, k = step[0], int(step[1:])
        if kind == "W":
            into_relay[k], into_total[k] = weight_chunk(k)
        elif kind == "R":
            into_total[k] += relay_chunk(k, into_relay[k])
        elif kind == "S":
            sum_chunk(k, into_total[k])
            if k in BATCH_AFTER:
                received += exchange(BATCH_AFTER[k])
        elif kind == "G" and k == 1:
            gcopies, lcopies = latent_step()
        elif kind == "G" and k == 2:
            gcopies = gain_step(
                gcopies, g1, g2, x * NZ + z, [{X: i, Z: j} for i, j in XZ_OFFSETS], NT - 1
            )
        else:
            gcopies = gain_step(
                gcopies, g2, g3, y, [{Y: i} for i in Y_OFFSETS], NT - 1 + NX * NZ - 1
            )
    for copy in lcopies:
        copy.wait_recv()
    for copy in received:
        copy.wait_recv()
    for i in range(NX):
        total = None
        for j in range(NZ):
            if (i, j) == (0, 0):
                term = esend[x * NZ + z]
            else:
                term = ebuf[XZ_OFFSETS.index((i, j))]
            total = term if total is None else total + term
        column = pl.multiple_of(shifted(X, -i) * BLOCK, BLOCK)
        weight_out[:, pl.ds(column, BLOCK)] = total * factor
    for copy in gcopies:
        copy.wait_recv()
    total = g3[0]
    for n in range(1, NY):
        total = total + g3[n]
    gain_out[...] = total * factor
    for copy in sends:
        copy.wait_send()


def store(*refs):
    for source, target in zip(refs[:3], refs[3:]):
        target[...] = source[...]


def per_device(latent_raw, norm_gain, up_weight, grad_kv):
    factor = float(latent_raw.shape[0] * NX * NY * NZ) ** (-0.5)
    vmem = pl.BlockSpec(memory_space=pltpu.VMEM)
    hbm = pl.BlockSpec(memory_space=pl.ANY)
    dma = pltpu.SemaphoreType.DMA
    gains = NT - 1 + NX * NZ - 1 + NY - 1
    chunks = len(CHUNKS)
    shapes = (
        jax.ShapeDtypeStruct((ROWS, KVL), jnp.bfloat16),
        jax.ShapeDtypeStruct((1, KVL), jnp.float32),
        jax.ShapeDtypeStruct((OWN, COLS), jnp.float32),
    )
    results = pl.pallas_call(
        functools.partial(kernel, factor),
        out_shape=shapes,
        in_specs=[hbm, hbm, hbm, hbm],
        out_specs=(vmem, vmem, vmem),
        scratch_shapes=[
            pltpu.VMEM((ROWS, KVL), jnp.bfloat16),
            pltpu.VMEM((1, KVL), jnp.float32),
            pltpu.VMEM((KVL, COLS), jnp.bfloat16),
            pltpu.VMEM((ROWS, COLS), jnp.bfloat16),
            pltpu.VMEM((NX * ROWS, KVL), jnp.bfloat16),
            pltpu.VMEM((NX * ROWS, BLOCK), jnp.bfloat16),
            pltpu.VMEM((KVL, BLOCK), jnp.float32),
            pltpu.VMEM((5, PIECE, BLOCK), jnp.bfloat16),
            pltpu.VMEM((2, PIECE, BLOCK), jnp.bfloat16),
            pltpu.VMEM((2, PIECE, BLOCK), jnp.bfloat16),
            pltpu.VMEM((2, PIECE // 2, BLOCK), jnp.bfloat16),
            pltpu.VMEM((2, PIECE, BLOCK), jnp.bfloat16),
            pltpu.VMEM((2, PIECE, BLOCK), jnp.bfloat16),
            pltpu.VMEM((NX * NZ, OWN, BLOCK), jnp.float32),
            pltpu.VMEM((NX * NZ - 1, OWN, BLOCK), jnp.float32),
            pltpu.VMEM((ROWS, KVL), jnp.float32),
            pltpu.VMEM((NT - 1, PART, KVL), jnp.float32),
            pltpu.VMEM((NT, 1, KVL), jnp.float32),
            pltpu.VMEM((NX * NZ, 1, KVL), jnp.float32),
            pltpu.VMEM((NY, 1, KVL), jnp.float32),
            dma((5,)),
            dma((NX - 1,)),
            dma((NX - 1,)),
            dma((NX - 1,)),
            dma((NX - 1,)),
            dma((NX - 1, chunks)),
            dma((NX - 1, chunks)),
            dma((8, chunks)),
            dma((8, chunks)),
            dma((NX * NZ - 1, len(BATCHES))),
            dma((NX * NZ - 1, len(BATCHES))),
            dma((NT - 1,)),
            dma((NT - 1,)),
            dma((NT - 1,)),
            dma((NT - 1,)),
            dma((gains,)),
            dma((gains,)),
        ],
        compiler_params=pltpu.CompilerParams(collective_id=0, has_side_effects=True),
        name="norm_up_backward",
    )(latent_raw, norm_gain.reshape(1, KVL), up_weight, grad_kv)
    latent_grad, gain_grad, weight_grad = pl.pallas_call(
        store, out_shape=shapes, in_specs=[vmem] * 3, out_specs=(vmem,) * 3, name="store",
    )(*results)
    return latent_grad, gain_grad.reshape(KVL), weight_grad


def solution(mesh):
    split = Mesh(mesh.devices.reshape(NX, NY, NZ, NH, NC), AXES)
    in_specs = (P(DP, None), P(), P(None, TENSOR), P(DP, TENSOR))
    out_specs = (P(DP, None), P(), P(DP, TENSOR))
    return jax.shard_map(
        per_device, mesh=split, in_specs=in_specs, out_specs=out_specs, check_vma=False
    )
```

time: 73.7 us -> 60.9 us (0.83)
  Pallas kernels: 68.4 us -> 60.2 us
  local copies, waits for them, and re-layouts: 4.34 us -> 0 us
    pallas_call x1 -> x2, Pallas kernels: 68.4 us -> 60.2 us  [the longest x1 58.5 us: per_device(): pl.pallas_call(functools.partial(kernel, factor), out_shape=shapes, in_sp...]
    unnamed x3 -> x0, local copies, waits for them, and re-layouts: 4.34 us -> none
where the time goes in v2:
time: 60.9 us; the launch traced here: 60.8 us
  Pallas kernels  60.2 us (99%)
  between operations  0.64 us (1%)
    pallas_call x1, Pallas kernels, per_device(): pl.pallas_call(functools.partial(kernel, factor), out_shape=shapes, in_sp...  58.5 us
    pallas_call x1, Pallas kernels, per_device(): pl.pallas_call(store, out_shape=shapes, in_specs=[vmem] * 3, out_specs=(v...  1.65 us

profile of v2, /device:TPU:6, one launch (start us, length us, event | category | flops | bytes accessed | tf_op | source)
XLA Modules:
  0.0 60.8 jit_solution(15126138646443357774)
XLA Ops:
  0.6 58.5 %norm_up_backward.1 = (bf16[192,512]{1,0:T(8,128)(2,1)}, f32[1,512]{1,0:T(1,128)}, f32[4,4096]{1,0:T(4,128)}) custom-call(bf16[192,512]{1,0:T(8,128)(2,1)} %latent_hbm.1, f32[1,512]{1,0:T(1,128)} %bitcast.2, bf16[512,4096]{1,0:T(8,128)(2,1)} %up_hbm.1, bf16[192,4096]{1,0:T(8,128)(2,1)} %grad_hbm.1), custom_call_target="tpu_custom_call" | custom-call | tf_op jit(solution)/shard_map/norm_up_backward/pallas_call | solution.py:332
  59.1 1.6 %store.1 = (bf16[192,512]{1,0:T(8,128)(2,1)}, f32[1,512]{1,0:T(1,128)}, f32[4,4096]{1,0:T(4,128)}) custom-call(bf16[192,512]{1,0:T(8,128)(2,1)} %get-tuple-element.9.refs_0_, f32[1,512]{1,0:T(1,128)} %get-tuple-element.10.refs_1_, f32[4,4096]{1,0:T(4,128)} %get-tuple-element.11.refs_2_), custom_call_target="tpu_custom_call" | custom-call | tf_op jit(solution)/shard_map/store/pallas_call | solution.py:379

commit v3 on v2

--- a/solution.py
+++ b/solution.py
@@ -28,7 +28,10 @@
 CHUNKS = ((0, 256), (256, 256), (512, 256), (768, 128), (896, 128))
 BATCHES = ((0, 512), (512, 384), (896, 128))
 BATCH_AFTER = {1: 0, 3: 1, 4: 2}
-SCHEDULE = "W0 W1 R0 G1 W2 R1 S0 W3 G2 W4 R2 S1 R3 R4 G3 S2 S3 S4"
+SCHEDULE = (
+    ("W", 0), ("W", 1), ("R", 0), ("W", 2), ("G", 1), ("R", 1), ("S", 0), ("W", 3), ("W", 4),
+    ("R", 2), ("S", 1), ("R", 3), ("G", 2), ("R", 4), ("S", 2), ("S", 3), ("S", 4), ("G", 3), ("L", 0),
+)
 HALF = ROWS // NC
 PIECE = OWN * NZ * NX
 
@@ -57,8 +60,8 @@
     latent_hbm, gain_hbm, up_hbm, grad_hbm,
     latent_out, gain_out, weight_out,
     latent, gain, up, grad, normed, tokens, full, wsend, direct, far, farther, rsend, relayed,
-    esend, ebuf, tsend, tbuf, g1, g2, g3,
-    local_sem, ns, nr, fs, fr, xs, xr, ys, yr, es, er, ts, tr, ls, lr, gs, gr,
+    esend, ebuf, tsend, tpair, tsum, tbuf, g1, g2, g3,
+    local_sem, ns, nr, fs, fr, xs, xr, ys, yr, es, er, ps, pr, ts, tr, ls, lr, gs, gr,
 ):
     x, y, z = (lax.axis_index(a) for a in DP)
     core = lax.axis_index(C)
@@ -122,21 +125,25 @@
     loads[4].wait()
     tsend[...] = lax.dot_general(
         grad[...], up[...], (((1,), (1,)), ((), ())), preferred_element_type=jnp.float32
+    ).reshape(NH, NC, PART, KVL)
+    sibling = at(**{C: 1})
+    tpaired = send(
+        tsend.at[:, lax.rem(core + 1, NC)], tpair, ps.at[0], pr.at[0], sibling
     )
-    tsends = []
-    for n, (i, j) in enumerate(T_OFFSETS):
-        other = shifted(H, i) * NC + shifted(C, j)
-        tsends.append(send(
-            tsend.at[pl.ds(pl.multiple_of(other * PART, PART), PART), :], tbuf.at[n],
-            ts.at[n], tr.at[n], at(**{H: i, C: j}),
-        ))
     loads[3].wait()
     forwards = []
     for n, i in enumerate(X_OFFSETS):
         halves[n].wait_recv()
         forwards.append(send(
-            normed.at[half(i), :], normed.at[half(i), :], fs.at[n], fr.at[n], at(**{C: 1})
+            normed.at[half(i), :], normed.at[half(i), :], fs.at[n], fr.at[n], sibling
         ))
+    tpaired.wait_recv()
+    for h in range(NH):
+        tsum[h] = tsend[h, core] + tpair[h]
+    tsends = [
+        send(tsum.at[shifted(H, i)], tbuf.at[i - 1], ts.at[i - 1], tr.at[i - 1], at(**{H: i}))
+        for i in range(1, NH)
+    ]
 
     def rows_of(other, p):
         return pl.ds(pl.multiple_of(128 * p + STRIP * other, STRIP), STRIP)
@@ -231,8 +238,8 @@
         for copy in tsends:
             copy.wait_recv()
         own = pl.ds(pl.multiple_of(t * PART, PART), PART)
-        grad_norm = tsend[own, :]
-        for n in range(NT - 1):
+        grad_norm = tsum[lax.axis_index(H)]
+        for n in range(NH - 1):
             grad_norm = grad_norm + tbuf[n]
         scaled, inverse = normalize(latent[own, :])
         g1[t] = jnp.sum(grad_norm * scaled, axis=0, keepdims=True)
@@ -244,13 +251,24 @@
             copies.append(send(
                 g1.at[t], g1.at[t], gs.at[n], gr.at[n], at(**{H: i, C: j})
             ))
-        lcopies = []
-        for n, (i, j) in enumerate(T_OFFSETS):
-            lcopies.append(send(
-                latent_out.at[own, :], latent_out.at[own, :], ls.at[n], lr.at[n],
-                at(**{H: i, C: j}),
-            ))
+        lcopies = [
+            send(
+                latent_out.at[own, :], latent_out.at[own, :], ls.at[n], lr.at[n], device
+            )
+            for n, device in enumerate((at(**{H: 1}), at(**{H: 2}), sibling))
+        ]
         return copies, lcopies
+
+    def forward_step(lcopies):
+        copies = lcopies[2:]
+        for n, i in enumerate((1, 2)):
+            lcopies[n].wait_recv()
+            part = shifted(H, -i) * NC + core
+            rows = pl.ds(pl.multiple_of(part * PART, PART), PART)
+            copies.append(send(
+                latent_out.at[rows, :], latent_out.at[rows, :], ls.at[3 + n], lr.at[3 + n], sibling
+            ))
+        return copies
 
     def gain_step(copies, source, target, slot, offsets, first):
         for copy in copies:
@@ -268,8 +286,7 @@
 
     into_relay, into_total, received = {}, {}, []
     gcopies = lcopies = None
-    for step in SCHEDULE.split():
-        kind, k = step[0], int(step[1:])
+    for kind, k in SCHEDULE:
         if kind == "W":
             into_relay[k], into_total[k] = weight_chunk(k)
         elif kind == "R":
@@ -280,6 +297,8 @@
                 received += exchange(BATCH_AFTER[k])
         elif kind == "G" and k == 1:
             gcopies, lcopies = latent_step()
+        elif kind == "L":
+            lcopies = forward_step(lcopies)
         elif kind == "G" and k == 2:
             gcopies = gain_step(
                 gcopies, g1, g2, x * NZ + z, [{X: i, Z: j} for i, j in XZ_OFFSETS], NT - 1
@@ -350,8 +369,10 @@
             pltpu.VMEM((2, PIECE, BLOCK), jnp.bfloat16),
             pltpu.VMEM((NX * NZ, OWN, BLOCK), jnp.float32),
             pltpu.VMEM((NX * NZ - 1, OWN, BLOCK), jnp.float32),
-            pltpu.VMEM((ROWS, KVL), jnp.float32),
-            pltpu.VMEM((NT - 1, PART, KVL), jnp.float32),
+            pltpu.VMEM((NH, NC, PART, KVL), jnp.float32),
+            pltpu.VMEM((NH, PART, KVL), jnp.float32),
+            pltpu.VMEM((NH, PART, KVL), jnp.float32),
+            pltpu.VMEM((NH - 1, PART, KVL), jnp.float32),
             pltpu.VMEM((NT, 1, KVL), jnp.float32),
             pltpu.VMEM((NX * NZ, 1, KVL), jnp.float32),
             pltpu.VMEM((NY, 1, KVL), jnp.float32),
@@ -366,8 +387,10 @@
             dma((8, chunks)),
             dma((NX * NZ - 1, len(BATCHES))),
             dma((NX * NZ - 1, len(BATCHES))),
-            dma((NT - 1,)),
-            dma((NT - 1,)),
+            dma((1,)),
+            dma((1,)),
+            dma((NH - 1,)),
+            dma((NH - 1,)),
             dma((NT - 1,)),
             dma((NT - 1,)),
             dma((gains,)),

time: 60.9 us -> 60.9 us (level)
  no operation moved by 1% of the time
where the time goes in v3:
time: 60.9 us; the launch traced here: 60.7 us
  Pallas kernels  60.1 us (99%)
  between operations  0.64 us (1%)
    pallas_call x1, Pallas kernels, per_device(): pl.pallas_call(functools.partial(kernel, factor), out_shape=shapes, in_sp...  58.5 us
    pallas_call x1, Pallas kernels, per_device(): pl.pallas_call(store, out_shape=shapes, in_specs=[vmem] * 3, out_specs=(v...  1.65 us

profile of v3, /device:TPU:6, one launch (start us, length us, event | category | flops | bytes accessed | tf_op | source)
XLA Modules:
  0.0 60.7 jit_solution(9959907383282982440)
XLA Ops:
  0.6 58.5 %norm_up_backward.1 = (bf16[192,512]{1,0:T(8,128)(2,1)}, f32[1,512]{1,0:T(1,128)}, f32[4,4096]{1,0:T(4,128)}) custom-call(bf16[192,512]{1,0:T(8,128)(2,1)} %latent_hbm.1, f32[1,512]{1,0:T(1,128)} %bitcast.2, bf16[512,4096]{1,0:T(8,128)(2,1)} %up_hbm.1, bf16[192,4096]{1,0:T(8,128)(2,1)} %grad_hbm.1), custom_call_target="tpu_custom_call" | custom-call | tf_op jit(solution)/shard_map/norm_up_backward/pallas_call | solution.py:351
  59.1 1.6 %store.1 = (bf16[192,512]{1,0:T(8,128)(2,1)}, f32[1,512]{1,0:T(1,128)}, f32[4,4096]{1,0:T(4,128)}) custom-call(bf16[192,512]{1,0:T(8,128)(2,1)} %get-tuple-element.9.refs_0_, f32[1,512]{1,0:T(1,128)} %get-tuple-element.10.refs_1_, f32[4,4096]{1,0:T(4,128)} %get-tuple-element.11.refs_2_), custom_call_target="tpu_custom_call" | custom-call | tf_op jit(solution)/shard_map/store/pallas_call | solution.py:402
